TPU v7x, 32 devices: a whole 2x2x4 slice. The times are simulated.
32 devices in a mesh: mkt: 4 (over z), prod: 2 (over core), draw: 4 (over y, x).
Axes of the slice: x: 2, y: 2, z: 4, core: 2. Of those that a mesh axis runs over, the one named last changes fastest.
Arguments:
- start_utility: float32 [1024, 256], P('mkt', 'prod'), may hold values from -5 to -2
- log_shares: float32 [1024, 256], P('mkt', 'prod'), may hold values from -9 to -5
- characteristics: float32 [1024, 8, 256], P('mkt', None, 'prod'), may hold values from -2.5 to 2.5
- coef_scale: float32 [8], replicated, may hold values from 0.1 to 0.3
- taste_draws: float32 [1024, 8, 2048], P('mkt', None, 'draw'), may hold values from -2.5 to 2.5
Outputs:
- mean_utility: float32 [1024, 256], P('mkt', 'prod')
- step_norms: float32 [2], replicated
All inputs are finite; a program needn't handle non-finite values.
Results may differ from a plain program's by a relative error of at most 0.0001.
Values sent between devices are 32-bit elements; how exact they have to be, the bound alone decides.
A program may use at most 64 MiB of HBM per device.

v0:
```python
import math
import jax
import jax.numpy as jnp
from jax import lax
from jax.sharding import PartitionSpec as P

R = 2048
ITERS = 2


def exponent(chars_part, scaled_part, util_part):
    spread = jnp.einsum("mkj,mkr->mjr", chars_part, scaled_part, precision=lax.Precision.HIGHEST)
    return jnp.exp(util_part[:, :, None] + spread)


def shards(start_utility, log_shares, characteristics, coef_scale, taste_draws):
    markets, coef_count, local_prod = characteristics.shape
    local_draws = taste_draws.shape[2]
    scaled = taste_draws * coef_scale[None, :, None]
    block_size = math.gcd(markets, 32)
    block_count = markets // block_size
    scaled_blocks = scaled.reshape(block_count, block_size, coef_count, local_draws)
    all_chars = lax.all_gather(characteristics, "prod", axis=2, tiled=True)
    all_blocks = all_chars.reshape(block_count, block_size, coef_count, -1)
    offset = lax.axis_index("prod") * local_prod
    utility = start_utility
    norm_list = []
    for iteration in range(ITERS):
        full_utility = lax.all_gather(utility, "prod", axis=1, tiled=True)

        def whole_pass(inputs):
            chars_part, scaled_part, util_part = inputs
            exp_util = exponent(chars_part, scaled_part, util_part)
            denominator = 1.0 + jnp.sum(exp_util, axis=1, keepdims=True)
            own_part = lax.dynamic_slice_in_dim(exp_util, offset, local_prod, 1)
            return jnp.sum(own_part / denominator, axis=2)

        summed = lax.map(
            whole_pass,
            (all_blocks, scaled_blocks, full_utility.reshape(block_count, block_size, -1)),
        )
        predicted = lax.psum(summed.reshape(markets, local_prod), "draw") / R
        updated = utility + log_shares - jnp.log(predicted)
        change = updated - utility
        square_sum = jnp.sum(change * change)
        norm_list.append(lax.psum(square_sum, ("mkt", "prod")))
        utility = updated
    totals = jnp.stack(norm_list)
    cell_count = markets * local_prod * lax.axis_size("mkt") * lax.axis_size("prod")
    step_norms = jnp.sqrt(totals / cell_count + 1e-06)
    return (utility, step_norms)


def solution(mesh):
    return jax.shard_map(
        shards,
        mesh=mesh,
        in_specs=(
            P("mkt", "prod"),
            P("mkt", "prod"),
            P("mkt", None, "prod"),
            P(),
            P("mkt", None, "draw"),
        ),
        out_specs=(P("mkt", "prod"), P()),
        check_vma=False,
    )
```

profile of v0, /device:TPU:0, one launch (start us, length us, event | category | flops | bytes accessed | tf_op | source)
XLA Modules:
  0.0 413.3 jit_solution(8134202163170635806)
XLA Ops:
  7.9 2.3 all_gather.9
  10.3 4.7 %broadcast_multiply_fusion = f32[256,8,512]{2,1,0:T(8,128)} fusion(f32[256,8,512]{2,1,0:T(8,128)} %param.13, f32[8]{0:T(128)} %param.12), kind=kLoop, calls=%fused_computation.22 | loop fusion | flops 1048576 | bytes 8388640 | tf_op jit(solution)/shard_map/mul | solution.py:19
  15.0 7.4 %all-gather.2.cloned.1.call-done = f32[256,8,256]{2,1,0:T(8,128)} async-done(((f32[256,8,128]{2,1,0:T(8,128)}), f32[256,8,256]{2,1,0:T(8,128)}) %all-gather.2.cloned.1.call-update) | async-done | bytes 2097168 | tf_op jit(solution)/shard_map/all_gather | solution.py:23
  22.4 136.7 %while.24 = (s32[]{:T(128)}, f32[8,32,128]{2,1,0:T(8,128)S(1)}, f32[8,32,256]{2,1,0:T(8,128)S(1)}, f32[8,32,8,256]{3,2,1,0:T(8,128)}, f32[8,32,8,512]{3,2,1,0:T(8,128)}, /*index=5*/s32[]{:T(128)}, s32[]{:T(128)}) while((s32[]{:T(128)}, f32[8,32,128]{2,1,0:T(8,128)S(1)}, f32[8,32,256]{2,1,0:T(8,128)S(1)}, f32[8,32,8,256]{3,2,1,0:T(8,128)}, ...), condition=%wide.region_3.4_spmd, body=%wide.region_0.3_spmd.sunk | while | flops 415232000 | bytes 26362968 | solution.py:38
  22.4 16.4 %fusion.20 = (f32[32,512]{1,0:T(8,128)S(1)}, f32[32,256,512]{2,1,0:T(8,128)S(1)}) fusion(f32[8,32,8,512]{3,2,1,0:T(8,128)} %get-tuple-element.285, s32[]{:T(128)} %get-tuple-element.274, f32[8,32,8,256]{3,2,1,0:T(8,128)} %get-tuple-element.284, f32[32,256]{1,0:T(8,128)S(1)} %dynamic-slice_bitcast_fusion.4), kind=kOutput, calls=%fused_computation.30.clone.1 | convolution fusion | flops 411025408 | bytes 17662976 | tf_op jit(solution)/shard_map/while/body/eval_jaxpr/mkj,mkr->mjr/dot_general | solution.py:12
  39.6 16.3 %fusion.20 = (f32[32,512]{1,0:T(8,128)S(1)}, f32[32,256,512]{2,1,0:T(8,128)S(1)}) fusion(f32[8,32,8,512]{3,2,1,0:T(8,128)} %get-tuple-element.285, s32[]{:T(128)} %get-tuple-element.274, f32[8,32,8,256]{3,2,1,0:T(8,128)} %get-tuple-element.284, f32[32,256]{1,0:T(8,128)S(1)} %dynamic-slice_bitcast_fusion.4), kind=kOutput, calls=%fused_computation.30.clone.1 | convolution fusion | flops 411025408 | bytes 17662976 | tf_op jit(solution)/shard_map/while/body/eval_jaxpr/mkj,mkr->mjr/dot_general | solution.py:12
  56.7 16.3 %fusion.20 = (f32[32,512]{1,0:T(8,128)S(1)}, f32[32,256,512]{2,1,0:T(8,128)S(1)}) fusion(f32[8,32,8,512]{3,2,1,0:T(8,128)} %get-tuple-element.285, s32[]{:T(128)} %get-tuple-element.274, f32[8,32,8,256]{3,2,1,0:T(8,128)} %get-tuple-element.284, f32[32,256]{1,0:T(8,128)S(1)} %dynamic-slice_bitcast_fusion.4), kind=kOutput, calls=%fused_computation.30.clone.1 | convolution fusion | flops 411025408 | bytes 17662976 | tf_op jit(solution)/shard_map/while/body/eval_jaxpr/mkj,mkr->mjr/dot_general | solution.py:12
  73.7 16.3 %fusion.20 = (f32[32,512]{1,0:T(8,128)S(1)}, f32[32,256,512]{2,1,0:T(8,128)S(1)}) fusion(f32[8,32,8,512]{3,2,1,0:T(8,128)} %get-tuple-element.285, s32[]{:T(128)} %get-tuple-element.274, f32[8,32,8,256]{3,2,1,0:T(8,128)} %get-tuple-element.284, f32[32,256]{1,0:T(8,128)S(1)} %dynamic-slice_bitcast_fusion.4), kind=kOutput, calls=%fused_computation.30.clone.1 | convolution fusion | flops 411025408 | bytes 17662976 | tf_op jit(solution)/shard_map/while/body/eval_jaxpr/mkj,mkr->mjr/dot_general | solution.py:12
  90.8 16.3 %fusion.20 = (f32[32,512]{1,0:T(8,128)S(1)}, f32[32,256,512]{2,1,0:T(8,128)S(1)}) fusion(f32[8,32,8,512]{3,2,1,0:T(8,128)} %get-tuple-element.285, s32[]{:T(128)} %get-tuple-element.274, f32[8,32,8,256]{3,2,1,0:T(8,128)} %get-tuple-element.284, f32[32,256]{1,0:T(8,128)S(1)} %dynamic-slice_bitcast_fusion.4), kind=kOutput, calls=%fused_computation.30.clone.1 | convolution fusion | flops 411025408 | bytes 17662976 | tf_op jit(solution)/shard_map/while/body/eval_jaxpr/mkj,mkr->mjr/dot_general | solution.py:12
  107.9 16.3 %fusion.20 = (f32[32,512]{1,0:T(8,128)S(1)}, f32[32,256,512]{2,1,0:T(8,128)S(1)}) fusion(f32[8,32,8,512]{3,2,1,0:T(8,128)} %get-tuple-element.285, s32[]{:T(128)} %get-tuple-element.274, f32[8,32,8,256]{3,2,1,0:T(8,128)} %get-tuple-element.284, f32[32,256]{1,0:T(8,128)S(1)} %dynamic-slice_bitcast_fusion.4), kind=kOutput, calls=%fused_computation.30.clone.1 | convolution fusion | flops 411025408 | bytes 17662976 | tf_op jit(solution)/shard_map/while/body/eval_jaxpr/mkj,mkr->mjr/dot_general | solution.py:12
  125.0 16.3 %fusion.20 = (f32[32,512]{1,0:T(8,128)S(1)}, f32[32,256,512]{2,1,0:T(8,128)S(1)}) fusion(f32[8,32,8,512]{3,2,1,0:T(8,128)} %get-tuple-element.285, s32[]{:T(128)} %get-tuple-element.274, f32[8,32,8,256]{3,2,1,0:T(8,128)} %get-tuple-element.284, f32[32,256]{1,0:T(8,128)S(1)} %dynamic-slice_bitcast_fusion.4), kind=kOutput, calls=%fused_computation.30.clone.1 | convolution fusion | flops 411025408 | bytes 17662976 | tf_op jit(solution)/shard_map/while/body/eval_jaxpr/mkj,mkr->mjr/dot_general | solution.py:12
  142.0 16.3 %fusion.20 = (f32[32,512]{1,0:T(8,128)S(1)}, f32[32,256,512]{2,1,0:T(8,128)S(1)}) fusion(f32[8,32,8,512]{3,2,1,0:T(8,128)} %get-tuple-element.285, s32[]{:T(128)} %get-tuple-element.274, f32[8,32,8,256]{3,2,1,0:T(8,128)} %get-tuple-element.284, f32[32,256]{1,0:T(8,128)S(1)} %dynamic-slice_bitcast_fusion.4), kind=kOutput, calls=%fused_computation.30.clone.1 | convolution fusion | flops 411025408 | bytes 17662976 | tf_op jit(solution)/shard_map/while/body/eval_jaxpr/mkj,mkr->mjr/dot_general | solution.py:12
  159.8 43.5 %all-reduce.4.cloned.1.call-done = f32[256,128]{1,0:T(8,128)} async-done(((f32[256,128]{1,0:T(8,128)}), f32[256,128]{1,0:T(8,128)}) %all-reduce.4.cloned.1.call-update) | async-done | bytes 131088 | tf_op jit(solution)/shard_map/psum | solution.py:42
  206.3 136.8 %while.25 = (s32[]{:T(128)}, f32[8,32,128]{2,1,0:T(8,128)S(1)}, f32[8,32,256]{2,1,0:T(8,128)S(1)}, f32[8,32,8,256]{3,2,1,0:T(8,128)}, f32[8,32,8,512]{3,2,1,0:T(8,128)}, /*index=5*/s32[]{:T(128)}, s32[]{:T(128)}) while((s32[]{:T(128)}, f32[8,32,128]{2,1,0:T(8,128)S(1)}, f32[8,32,256]{2,1,0:T(8,128)S(1)}, f32[8,32,8,256]{3,2,1,0:T(8,128)}, ...), condition=%wide.region_8.9_spmd, body=%wide.region_5.8_spmd.sunk | while | flops 415232000 | bytes 26362968 | solution.py:38
  206.5 16.3 %fusion.22 = (f32[32,512]{1,0:T(8,128)S(1)}, f32[32,256,512]{2,1,0:T(8,128)S(1)}) fusion(f32[8,32,8,512]{3,2,1,0:T(8,128)} %get-tuple-element.306, s32[]{:T(128)} %get-tuple-element.295, f32[8,32,8,256]{3,2,1,0:T(8,128)} %get-tuple-element.305, f32[32,256]{1,0:T(8,128)S(1)} %dynamic-slice_bitcast_fusion.5), kind=kOutput, calls=%fused_computation.31.clone.1 | convolution fusion | flops 411025408 | bytes 17662976 | tf_op jit(solution)/shard_map/while/body/eval_jaxpr/mkj,mkr->mjr/dot_general | solution.py:12
  223.6 16.3 %fusion.22 = (f32[32,512]{1,0:T(8,128)S(1)}, f32[32,256,512]{2,1,0:T(8,128)S(1)}) fusion(f32[8,32,8,512]{3,2,1,0:T(8,128)} %get-tuple-element.306, s32[]{:T(128)} %get-tuple-element.295, f32[8,32,8,256]{3,2,1,0:T(8,128)} %get-tuple-element.305, f32[32,256]{1,0:T(8,128)S(1)} %dynamic-slice_bitcast_fusion.5), kind=kOutput, calls=%fused_computation.31.clone.1 | convolution fusion | flops 411025408 | bytes 17662976 | tf_op jit(solution)/shard_map/while/body/eval_jaxpr/mkj,mkr->mjr/dot_general | solution.py:12
  240.7 16.3 %fusion.22 = (f32[32,512]{1,0:T(8,128)S(1)}, f32[32,256,512]{2,1,0:T(8,128)S(1)}) fusion(f32[8,32,8,512]{3,2,1,0:T(8,128)} %get-tuple-element.306, s32[]{:T(128)} %get-tuple-element.295, f32[8,32,8,256]{3,2,1,0:T(8,128)} %get-tuple-element.305, f32[32,256]{1,0:T(8,128)S(1)} %dynamic-slice_bitcast_fusion.5), kind=kOutput, calls=%fused_computation.31.clone.1 | convolution fusion | flops 411025408 | bytes 17662976 | tf_op jit(solution)/shard_map/while/body/eval_jaxpr/mkj,mkr->mjr/dot_general | solution.py:12
  257.7 16.3 %fusion.22 = (f32[32,512]{1,0:T(8,128)S(1)}, f32[32,256,512]{2,1,0:T(8,128)S(1)}) fusion(f32[8,32,8,512]{3,2,1,0:T(8,128)} %get-tuple-element.306, s32[]{:T(128)} %get-tuple-element.295, f32[8,32,8,256]{3,2,1,0:T(8,128)} %get-tuple-element.305, f32[32,256]{1,0:T(8,128)S(1)} %dynamic-slice_bitcast_fusion.5), kind=kOutput, calls=%fused_computation.31.clone.1 | convolution fusion | flops 411025408 | bytes 17662976 | tf_op jit(solution)/shard_map/while/body/eval_jaxpr/mkj,mkr->mjr/dot_general | solution.py:12
  274.8 16.3 %fusion.22 = (f32[32,512]{1,0:T(8,128)S(1)}, f32[32,256,512]{2,1,0:T(8,128)S(1)}) fusion(f32[8,32,8,512]{3,2,1,0:T(8,128)} %get-tuple-element.306, s32[]{:T(128)} %get-tuple-element.295, f32[8,32,8,256]{3,2,1,0:T(8,128)} %get-tuple-element.305, f32[32,256]{1,0:T(8,128)S(1)} %dynamic-slice_bitcast_fusion.5), kind=kOutput, calls=%fused_computation.31.clone.1 | convolution fusion | flops 411025408 | bytes 17662976 | tf_op jit(solution)/shard_map/while/body/eval_jaxpr/mkj,mkr->mjr/dot_general | solution.py:12
  291.9 16.3 %fusion.22 = (f32[32,512]{1,0:T(8,128)S(1)}, f32[32,256,512]{2,1,0:T(8,128)S(1)}) fusion(f32[8,32,8,512]{3,2,1,0:T(8,128)} %get-tuple-element.306, s32[]{:T(128)} %get-tuple-element.295, f32[8,32,8,256]{3,2,1,0:T(8,128)} %get-tuple-element.305, f32[32,256]{1,0:T(8,128)S(1)} %dynamic-slice_bitcast_fusion.5), kind=kOutput, calls=%fused_computation.31.clone.1 | convolution fusion | flops 411025408 | bytes 17662976 | tf_op jit(solution)/shard_map/while/body/eval_jaxpr/mkj,mkr->mjr/dot_general | solution.py:12
  309.0 16.3 %fusion.22 = (f32[32,512]{1,0:T(8,128)S(1)}, f32[32,256,512]{2,1,0:T(8,128)S(1)}) fusion(f32[8,32,8,512]{3,2,1,0:T(8,128)} %get-tuple-element.306, s32[]{:T(128)} %get-tuple-element.295, f32[8,32,8,256]{3,2,1,0:T(8,128)} %get-tuple-element.305, f32[32,256]{1,0:T(8,128)S(1)} %dynamic-slice_bitcast_fusion.5), kind=kOutput, calls=%fused_computation.31.clone.1 | convolution fusion | flops 411025408 | bytes 17662976 | tf_op jit(solution)/shard_map/while/body/eval_jaxpr/mkj,mkr->mjr/dot_general | solution.py:12
  326.1 16.3 %fusion.22 = (f32[32,512]{1,0:T(8,128)S(1)}, f32[32,256,512]{2,1,0:T(8,128)S(1)}) fusion(f32[8,32,8,512]{3,2,1,0:T(8,128)} %get-tuple-element.306, s32[]{:T(128)} %get-tuple-element.295, f32[8,32,8,256]{3,2,1,0:T(8,128)} %get-tuple-element.305, f32[32,256]{1,0:T(8,128)S(1)} %dynamic-slice_bitcast_fusion.5), kind=kOutput, calls=%fused_computation.31.clone.1 | convolution fusion | flops 411025408 | bytes 17662976 | tf_op jit(solution)/shard_map/while/body/eval_jaxpr/mkj,mkr->mjr/dot_general | solution.py:12
  343.8 42.4 %all-reduce.6.cloned.1.call-done = f32[256,128]{1,0:T(8,128)} async-done(((f32[256,128]{1,0:T(8,128)}), f32[256,128]{1,0:T(8,128)}) %all-reduce.6.cloned.1.call-update) | async-done | bytes 131088 | tf_op jit(solution)/shard_map/psum | solution.py:42
  388.4 16.6 %all-reduce = (f32[1]{0:T(128)}, f32[1]{0:T(128)}) all-reduce(f32[1]{0:T(128)} %bitcast.15, f32[1]{0:T(128)} %bitcast.14), channel_id=1, replica_groups=mesh['mkt'=4,'prod'=2,'draw'=4] {'mkt','prod'}, use_global_device_ids=true, to_apply=%region_13.14 | all-reduce | flops 2 | bytes 16 | tf_op jit(solution)/shard_map/psum | solution.py:46
  (84 shorter events, 20.2 us)
Async XLA Ops:
  7.2 15.2 %all-gather.2.cloned.1.call-start = ((), (), s32[]{:S(2)}) async-start(), calls=%async_computation | async-start | bytes 3145728 | tf_op jit(solution)/shard_map/all_gather | solution.py:23
  7.9 195.5 %all-reduce.4.cloned.1.call-start = ((), (), s32[]{:S(2)}) async-start(), calls=%async_computation.1 | async-start | bytes 262144 | tf_op jit(solution)/shard_map/psum | solution.py:42
  22.4 181.0 %copy-start = (f32[256,128]{1,0:T(8,128)S(1)}, f32[256,128]{1,0:T(8,128)}, u32[]{:S(2)}) copy-start(f32[256,128]{1,0:T(8,128)} %param.9) | copy-start | bytes 393220
  22.4 181.0 %copy-start.1 = (f32[256,128]{1,0:T(8,128)S(1)}, f32[256,128]{1,0:T(8,128)}, u32[]{:S(2)}) copy-start(f32[256,128]{1,0:T(8,128)} %param.10) | copy-start | bytes 393220
  159.1 0.7 copy-start.3
  159.8 226.4 %all-reduce.6.cloned.1.call-start = ((), (), s32[]{:S(2)}) async-start(), calls=%async_computation.2 | async-start | bytes 262144 | tf_op jit(solution)/shard_map/psum | solution.py:42
  343.1 0.7 copy-start.2
Sparse Core Ops, SparseCore 0:
  9.5 12.8 all-gather.1
  159.9 43.4 all-reduce.3
  343.9 42.1 all-reduce.5
where the time goes:
time: 414 us; the launch traced here: 413 us
  matrix products  261 us (63%)
  waiting for transfers between devices  94 us (23%)
  blocking collectives  20.9 us (5%)
  other arithmetic  20.5 us (5%)
  between operations  13.8 us (3%)
    dot_general x16, matrix products, exponent(): jnp.einsum('mkj,mkr->mjr', chars_part, scaled_part, precision=lax.Precisi...  261 us
    psum x2, waiting for transfers between devices, shards(): predicted = lax.psum(summed.reshape(markets, local_prod), 'draw') / R  85.9 us
    psum x1, blocking collectives, shards(): norm_list.append(lax.psum(square_sum, ('mkt', 'prod')))  16.6 us
    reduce_sum x16, other arithmetic, whole_pass(): return jnp.sum(own_part / denominator, axis=2)  10.7 us
  transfers between devices with their start and end apart: 3, of which 3 were waited for; matrix products, arithmetic and copies ran while one was open for 1% of the time, Pallas kernels for 0%

commit v1 on v0

--- a/solution.py
+++ b/solution.py
@@ -6,6 +6,11 @@
 
 R = 2048
 ITERS = 2
+
+
+def cut_loops(a0, axis_key="draw"):
+    fresh = jax.lax.all_gather(a0, axis_name=axis_key)
+    return jnp.sum(fresh, 0)
 
 
 def exponent(chars_part, scaled_part, util_part):
@@ -39,7 +44,7 @@
             whole_pass,
             (all_blocks, scaled_blocks, full_utility.reshape(block_count, block_size, -1)),
         )
-        predicted = lax.psum(summed.reshape(markets, local_prod), "draw") / R
+        predicted = cut_loops(summed.reshape(markets, local_prod)) / R
         updated = utility + log_shares - jnp.log(predicted)
         change = updated - utility
         square_sum = jnp.sum(change * change)

time: 414 us -> 344 us (0.83)
  waiting for transfers between devices: 94 us -> 8.12 us
  blocking collectives: 20.9 us -> 39.9 us
    psum x2 -> x0, waiting for transfers between devices: 85.9 us -> none  [shards(): predicted = lax.psum(summed.reshape(markets, local_prod), 'draw') / R]
    all_gather x0 -> x2, blocking collectives: none -> 20.3 us  [cut_loops(): fresh = jax.lax.all_gather(a0, axis_name=axis_key)]
  transfers between devices with their start and end apart: 3 -> 1, of which waited for: 3 -> 1; matrix products, arithmetic and copies ran while one was open for 1% -> 1% of each run, Pallas kernels for 0% -> 0%
where the time goes in v1:
time: 344 us
  matrix products  261 us (76%)
  blocking collectives  39.9 us (12%)
  other arithmetic  18.7 us (5%)
  between operations  14.1 us (4%)
  waiting for transfers between devices  8.12 us (2%)
    dot_general x16, matrix products, exponent(): jnp.einsum('mkj,mkr->mjr', chars_part, scaled_part, precision=lax.Precisi...  261 us
    all_gather x2, blocking collectives, cut_loops(): fresh = jax.lax.all_gather(a0, axis_name=axis_key)  20.3 us
    psum x1, blocking collectives, shards(): norm_list.append(lax.psum(square_sum, ('mkt', 'prod')))  15.3 us
    reduce_sum x16, other arithmetic, whole_pass(): return jnp.sum(own_part / denominator, axis=2)  10.7 us
    all_gather x1, waiting for transfers between devices, shards(): all_chars = lax.all_gather(characteristics, 'prod', axis=2, tiled=True)  7.44 us
  transfers between devices with their start and end apart: 1, of which 1 were waited for; matrix products, arithmetic and copies ran while one was open for 1% of the time, Pallas kernels for 0%

profile of v1, /device:TPU:0, one launch (start us, length us, event | category | flops | bytes accessed | tf_op | source)
XLA Modules:
  0.0 343.6 jit_solution(14407108026044058613)
XLA Ops:
  7.9 2.3 all_gather.15
  10.2 4.7 %broadcast_multiply_fusion = f32[256,8,512]{2,1,0:T(8,128)} fusion(f32[256,8,512]{2,1,0:T(8,128)} %param.13, f32[8]{0:T(128)} %param.12), kind=kLoop, calls=%fused_computation.22 | loop fusion | flops 1048576 | bytes 8388640 | tf_op jit(solution)/shard_map/mul | solution.py:24
  14.9 7.4 %all-gather.2.cloned.1.call-done = f32[256,8,256]{2,1,0:T(8,128)} async-done(((f32[256,8,128]{2,1,0:T(8,128)}), f32[256,8,256]{2,1,0:T(8,128)}) %all-gather.2.cloned.1.call-update) | async-done | bytes 2097168 | tf_op jit(solution)/shard_map/all_gather | solution.py:28
  22.4 136.7 %while.24 = (s32[]{:T(128)}, f32[8,32,128]{2,1,0:T(8,128)S(1)}, f32[8,32,256]{2,1,0:T(8,128)S(1)}, f32[8,32,8,256]{3,2,1,0:T(8,128)}, f32[8,32,8,512]{3,2,1,0:T(8,128)}, /*index=5*/s32[]{:T(128)}, s32[]{:T(128)}) while((s32[]{:T(128)}, f32[8,32,128]{2,1,0:T(8,128)S(1)}, f32[8,32,256]{2,1,0:T(8,128)S(1)}, f32[8,32,8,256]{3,2,1,0:T(8,128)}, ...), condition=%wide.region_3.4_spmd, body=%wide.region_0.3_spmd.sunk | while | flops 415232000 | bytes 26362968 | solution.py:43
  22.4 16.4 %fusion.20 = (f32[32,512]{1,0:T(8,128)S(1)}, f32[32,256,512]{2,1,0:T(8,128)S(1)}) fusion(f32[8,32,8,512]{3,2,1,0:T(8,128)} %get-tuple-element.285, s32[]{:T(128)} %get-tuple-element.274, f32[8,32,8,256]{3,2,1,0:T(8,128)} %get-tuple-element.284, f32[32,256]{1,0:T(8,128)S(1)} %dynamic-slice_bitcast_fusion.4), kind=kOutput, calls=%fused_computation.30.clone.1 | convolution fusion | flops 411025408 | bytes 17662976 | tf_op jit(solution)/shard_map/while/body/eval_jaxpr/mkj,mkr->mjr/dot_general | solution.py:17
  39.6 16.3 %fusion.20 = (f32[32,512]{1,0:T(8,128)S(1)}, f32[32,256,512]{2,1,0:T(8,128)S(1)}) fusion(f32[8,32,8,512]{3,2,1,0:T(8,128)} %get-tuple-element.285, s32[]{:T(128)} %get-tuple-element.274, f32[8,32,8,256]{3,2,1,0:T(8,128)} %get-tuple-element.284, f32[32,256]{1,0:T(8,128)S(1)} %dynamic-slice_bitcast_fusion.4), kind=kOutput, calls=%fused_computation.30.clone.1 | convolution fusion | flops 411025408 | bytes 17662976 | tf_op jit(solution)/shard_map/while/body/eval_jaxpr/mkj,mkr->mjr/dot_general | solution.py:17
  56.7 16.3 %fusion.20 = (f32[32,512]{1,0:T(8,128)S(1)}, f32[32,256,512]{2,1,0:T(8,128)S(1)}) fusion(f32[8,32,8,512]{3,2,1,0:T(8,128)} %get-tuple-element.285, s32[]{:T(128)} %get-tuple-element.274, f32[8,32,8,256]{3,2,1,0:T(8,128)} %get-tuple-element.284, f32[32,256]{1,0:T(8,128)S(1)} %dynamic-slice_bitcast_fusion.4), kind=kOutput, calls=%fused_computation.30.clone.1 | convolution fusion | flops 411025408 | bytes 17662976 | tf_op jit(solution)/shard_map/while/body/eval_jaxpr/mkj,mkr->mjr/dot_general | solution.py:17
  73.7 16.3 %fusion.20 = (f32[32,512]{1,0:T(8,128)S(1)}, f32[32,256,512]{2,1,0:T(8,128)S(1)}) fusion(f32[8,32,8,512]{3,2,1,0:T(8,128)} %get-tuple-element.285, s32[]{:T(128)} %get-tuple-element.274, f32[8,32,8,256]{3,2,1,0:T(8,128)} %get-tuple-element.284, f32[32,256]{1,0:T(8,128)S(1)} %dynamic-slice_bitcast_fusion.4), kind=kOutput, calls=%fused_computation.30.clone.1 | convolution fusion | flops 411025408 | bytes 17662976 | tf_op jit(solution)/shard_map/while/body/eval_jaxpr/mkj,mkr->mjr/dot_general | solution.py:17
  90.8 16.3 %fusion.20 = (f32[32,512]{1,0:T(8,128)S(1)}, f32[32,256,512]{2,1,0:T(8,128)S(1)}) fusion(f32[8,32,8,512]{3,2,1,0:T(8,128)} %get-tuple-element.285, s32[]{:T(128)} %get-tuple-element.274, f32[8,32,8,256]{3,2,1,0:T(8,128)} %get-tuple-element.284, f32[32,256]{1,0:T(8,128)S(1)} %dynamic-slice_bitcast_fusion.4), kind=kOutput, calls=%fused_computation.30.clone.1 | convolution fusion | flops 411025408 | bytes 17662976 | tf_op jit(solution)/shard_map/while/body/eval_jaxpr/mkj,mkr->mjr/dot_general | solution.py:17
  107.9 16.3 %fusion.20 = (f32[32,512]{1,0:T(8,128)S(1)}, f32[32,256,512]{2,1,0:T(8,128)S(1)}) fusion(f32[8,32,8,512]{3,2,1,0:T(8,128)} %get-tuple-element.285, s32[]{:T(128)} %get-tuple-element.274, f32[8,32,8,256]{3,2,1,0:T(8,128)} %get-tuple-element.284, f32[32,256]{1,0:T(8,128)S(1)} %dynamic-slice_bitcast_fusion.4), kind=kOutput, calls=%fused_computation.30.clone.1 | convolution fusion | flops 411025408 | bytes 17662976 | tf_op jit(solution)/shard_map/while/body/eval_jaxpr/mkj,mkr->mjr/dot_general | solution.py:17
  125.0 16.3 %fusion.20 = (f32[32,512]{1,0:T(8,128)S(1)}, f32[32,256,512]{2,1,0:T(8,128)S(1)}) fusion(f32[8,32,8,512]{3,2,1,0:T(8,128)} %get-tuple-element.285, s32[]{:T(128)} %get-tuple-element.274, f32[8,32,8,256]{3,2,1,0:T(8,128)} %get-tuple-element.284, f32[32,256]{1,0:T(8,128)S(1)} %dynamic-slice_bitcast_fusion.4), kind=kOutput, calls=%fused_computation.30.clone.1 | convolution fusion | flops 411025408 | bytes 17662976 | tf_op jit(solution)/shard_map/while/body/eval_jaxpr/mkj,mkr->mjr/dot_general | solution.py:17
  142.0 16.3 %fusion.20 = (f32[32,512]{1,0:T(8,128)S(1)}, f32[32,256,512]{2,1,0:T(8,128)S(1)}) fusion(f32[8,32,8,512]{3,2,1,0:T(8,128)} %get-tuple-element.285, s32[]{:T(128)} %get-tuple-element.274, f32[8,32,8,256]{3,2,1,0:T(8,128)} %get-tuple-element.284, f32[32,256]{1,0:T(8,128)S(1)} %dynamic-slice_bitcast_fusion.4), kind=kOutput, calls=%fused_computation.30.clone.1 | convolution fusion | flops 411025408 | bytes 17662976 | tf_op jit(solution)/shard_map/while/body/eval_jaxpr/mkj,mkr->mjr/dot_general | solution.py:17
  159.1 10.3 %all_gather.17 = f32[4,256,128]{2,1,0:T(8,128)S(1)} all-gather(f32[1,256,128]{2,1,0:T(8,128)S(1)} %bitcast.56), channel_id=1, replica_groups=mesh['mkt'=4,'prod'=2,'draw'=4] {'draw'}, dimensions={0}, use_global_device_ids=true | all-gather | bytes 655360 | tf_op jit(solution)/shard_map/all_gather | solution.py:12
  171.5 136.8 %while.25 = (s32[]{:T(128)}, f32[8,32,128]{2,1,0:T(8,128)S(1)}, f32[8,32,256]{2,1,0:T(8,128)S(1)}, f32[8,32,8,256]{3,2,1,0:T(8,128)}, f32[8,32,8,512]{3,2,1,0:T(8,128)}, /*index=5*/s32[]{:T(128)}, s32[]{:T(128)}) while((s32[]{:T(128)}, f32[8,32,128]{2,1,0:T(8,128)S(1)}, f32[8,32,256]{2,1,0:T(8,128)S(1)}, f32[8,32,8,256]{3,2,1,0:T(8,128)}, ...), condition=%wide.region_8.9_spmd, body=%wide.region_5.8_spmd.sunk | while | flops 415232000 | bytes 26362968 | solution.py:43
  171.7 16.3 %fusion.22 = (f32[32,512]{1,0:T(8,128)S(1)}, f32[32,256,512]{2,1,0:T(8,128)S(1)}) fusion(f32[8,32,8,512]{3,2,1,0:T(8,128)} %get-tuple-element.306, s32[]{:T(128)} %get-tuple-element.295, f32[8,32,8,256]{3,2,1,0:T(8,128)} %get-tuple-element.305, f32[32,256]{1,0:T(8,128)S(1)} %dynamic-slice_bitcast_fusion.5), kind=kOutput, calls=%fused_computation.31.clone.1 | convolution fusion | flops 411025408 | bytes 17662976 | tf_op jit(solution)/shard_map/while/body/eval_jaxpr/mkj,mkr->mjr/dot_general | solution.py:17
  188.8 16.3 %fusion.22 = (f32[32,512]{1,0:T(8,128)S(1)}, f32[32,256,512]{2,1,0:T(8,128)S(1)}) fusion(f32[8,32,8,512]{3,2,1,0:T(8,128)} %get-tuple-element.306, s32[]{:T(128)} %get-tuple-element.295, f32[8,32,8,256]{3,2,1,0:T(8,128)} %get-tuple-element.305, f32[32,256]{1,0:T(8,128)S(1)} %dynamic-slice_bitcast_fusion.5), kind=kOutput, calls=%fused_computation.31.clone.1 | convolution fusion | flops 411025408 | bytes 17662976 | tf_op jit(solution)/shard_map/while/body/eval_jaxpr/mkj,mkr->mjr/dot_general | solution.py:17
  205.9 16.3 %fusion.22 = (f32[32,512]{1,0:T(8,128)S(1)}, f32[32,256,512]{2,1,0:T(8,128)S(1)}) fusion(f32[8,32,8,512]{3,2,1,0:T(8,128)} %get-tuple-element.306, s32[]{:T(128)} %get-tuple-element.295, f32[8,32,8,256]{3,2,1,0:T(8,128)} %get-tuple-element.305, f32[32,256]{1,0:T(8,128)S(1)} %dynamic-slice_bitcast_fusion.5), kind=kOutput, calls=%fused_computation.31.clone.1 | convolution fusion | flops 411025408 | bytes 17662976 | tf_op jit(solution)/shard_map/while/body/eval_jaxpr/mkj,mkr->mjr/dot_general | solution.py:17
  222.9 16.3 %fusion.22 = (f32[32,512]{1,0:T(8,128)S(1)}, f32[32,256,512]{2,1,0:T(8,128)S(1)}) fusion(f32[8,32,8,512]{3,2,1,0:T(8,128)} %get-tuple-element.306, s32[]{:T(128)} %get-tuple-element.295, f32[8,32,8,256]{3,2,1,0:T(8,128)} %get-tuple-element.305, f32[32,256]{1,0:T(8,128)S(1)} %dynamic-slice_bitcast_fusion.5), kind=kOutput, calls=%fused_computation.31.clone.1 | convolution fusion | flops 411025408 | bytes 17662976 | tf_op jit(solution)/shard_map/while/body/eval_jaxpr/mkj,mkr->mjr/dot_general | solution.py:17
  240.0 16.3 %fusion.22 = (f32[32,512]{1,0:T(8,128)S(1)}, f32[32,256,512]{2,1,0:T(8,128)S(1)}) fusion(f32[8,32,8,512]{3,2,1,0:T(8,128)} %get-tuple-element.306, s32[]{:T(128)} %get-tuple-element.295, f32[8,32,8,256]{3,2,1,0:T(8,128)} %get-tuple-element.305, f32[32,256]{1,0:T(8,128)S(1)} %dynamic-slice_bitcast_fusion.5), kind=kOutput, calls=%fused_computation.31.clone.1 | convolution fusion | flops 411025408 | bytes 17662976 | tf_op jit(solution)/shard_map/while/body/eval_jaxpr/mkj,mkr->mjr/dot_general | solution.py:17
  257.1 16.3 %fusion.22 = (f32[32,512]{1,0:T(8,128)S(1)}, f32[32,256,512]{2,1,0:T(8,128)S(1)}) fusion(f32[8,32,8,512]{3,2,1,0:T(8,128)} %get-tuple-element.306, s32[]{:T(128)} %get-tuple-element.295, f32[8,32,8,256]{3,2,1,0:T(8,128)} %get-tuple-element.305, f32[32,256]{1,0:T(8,128)S(1)} %dynamic-slice_bitcast_fusion.5), kind=kOutput, calls=%fused_computation.31.clone.1 | convolution fusion | flops 411025408 | bytes 17662976 | tf_op jit(solution)/shard_map/while/body/eval_jaxpr/mkj,mkr->mjr/dot_general | solution.py:17
  274.2 16.3 %fusion.22 = (f32[32,512]{1,0:T(8,128)S(1)}, f32[32,256,512]{2,1,0:T(8,128)S(1)}) fusion(f32[8,32,8,512]{3,2,1,0:T(8,128)} %get-tuple-element.306, s32[]{:T(128)} %get-tuple-element.295, f32[8,32,8,256]{3,2,1,0:T(8,128)} %get-tuple-element.305, f32[32,256]{1,0:T(8,128)S(1)} %dynamic-slice_bitcast_fusion.5), kind=kOutput, calls=%fused_computation.31.clone.1 | convolution fusion | flops 411025408 | bytes 17662976 | tf_op jit(solution)/shard_map/while/body/eval_jaxpr/mkj,mkr->mjr/dot_general | solution.py:17
  291.3 16.3 %fusion.22 = (f32[32,512]{1,0:T(8,128)S(1)}, f32[32,256,512]{2,1,0:T(8,128)S(1)}) fusion(f32[8,32,8,512]{3,2,1,0:T(8,128)} %get-tuple-element.306, s32[]{:T(128)} %get-tuple-element.295, f32[8,32,8,256]{3,2,1,0:T(8,128)} %get-tuple-element.305, f32[32,256]{1,0:T(8,128)S(1)} %dynamic-slice_bitcast_fusion.5), kind=kOutput, calls=%fused_computation.31.clone.1 | convolution fusion | flops 411025408 | bytes 17662976 | tf_op jit(solution)/shard_map/while/body/eval_jaxpr/mkj,mkr->mjr/dot_general | solution.py:17
  308.3 10.0 %all_gather.19 = f32[4,256,128]{2,1,0:T(8,128)S(1)} all-gather(f32[1,256,128]{2,1,0:T(8,128)S(1)} %bitcast.57), channel_id=1, replica_groups=mesh['mkt'=4,'prod'=2,'draw'=4] {'draw'}, dimensions={0}, use_global_device_ids=true | all-gather | bytes 655360 | tf_op jit(solution)/shard_map/all_gather | solution.py:12
  319.7 15.3 %all-reduce = (f32[1]{0:T(128)}, f32[1]{0:T(128)}) all-reduce(f32[1]{0:T(128)} %bitcast.15, f32[1]{0:T(128)} %bitcast.14), channel_id=1, replica_groups=mesh['mkt'=4,'prod'=2,'draw'=4] {'mkt','prod'}, use_global_device_ids=true, to_apply=%region_13.14 | all-reduce | flops 2 | bytes 16 | tf_op jit(solution)/shard_map/psum | solution.py:51
  (78 shorter events, 17.1 us)
Async XLA Ops:
  7.2 15.2 %all-gather.2.cloned.1.call-start = ((), (), s32[]{:S(2)}) async-start(), calls=%async_computation | async-start | bytes 3145728 | tf_op jit(solution)/shard_map/all_gather | solution.py:28
  22.4 147.0 %copy-start = (f32[256,128]{1,0:T(8,128)S(1)}, f32[256,128]{1,0:T(8,128)}, u32[]{:S(2)}) copy-start(f32[256,128]{1,0:T(8,128)} %param.9) | copy-start | bytes 393220
  22.4 147.0 %copy-start.1 = (f32[256,128]{1,0:T(8,128)S(1)}, f32[256,128]{1,0:T(8,128)}, u32[]{:S(2)}) copy-start(f32[256,128]{1,0:T(8,128)} %param.10) | copy-start | bytes 393220
Sparse Core Ops, SparseCore 0:
  9.5 12.8 all-gather.1
